TPU v7x, 32 devices: a whole 2x2x4 slice. The times are simulated.
32 devices in a mesh: gx: 8 (over z, y), gy: 4 (over x, core).
Axes of the slice: x: 2, y: 2, z: 4, core: 2. Of those that a mesh axis runs over, the one named last changes fastest.
Arguments:
- state: float32 [4, 2, 4194304], P('gy', None, 'gx'), may hold values from -6 to 6
- fields: float32 [22], replicated, may hold values from 0.5 to 2
- couplings: float32 [22], replicated, may hold values from 0.5 to 2
- noise: float32 [4, 4, 2], P('gy'), may hold values from -5 to 5
Outputs:
- final_state: float32 [4, 2, 4194304], P('gy', None, 'gx')
- record: float32 [4, 2], replicated
All inputs are finite; a program needn't handle non-finite values.
Results may differ from a plain program's by a relative error of at most 0.0001.
Values sent between devices are 32-bit elements; how exact they have to be, the bound alone decides.
A program may use at most 128 MiB of HBM per device.

v0:
```python
import functools

import jax
import jax.numpy as jnp
from jax import lax
from jax.experimental import pallas as pl
from jax.experimental.pallas import tpu as pltpu
from jax.sharding import PartitionSpec as P

kappa_rate = 4.0
time_step = 0.05
LANES = 128
CHUNK = 64


def bit_spin(ids, q):
    return 1.0 - 2.0 * (ids >> q & 1).astype(jnp.float32)


def step_kernel(
    high_bits, spins, table, params, block_params, fields, flips, low_energy, own, *rest
):
    partners = rest[:high_bits]
    out, sums = rest[high_bits:]
    rows = own.shape[2]
    row_bits = rows.bit_length() - 1
    chunk_bits = CHUNK.bit_length() - 1
    g = pl.program_id(0)
    rate, factor, damp, kick_one, kick_two, magnet = (params[k] for k in range(6))
    high_ones, top_link, lane_link, high_energy = (block_params[g * 4 + k] for k in range(4))

    row_ids = lax.broadcasted_iota(jnp.int32, (CHUNK, LANES), 0)
    lane_ids = lax.broadcasted_iota(jnp.int32, (CHUNK, LANES), 1)
    ones = jnp.zeros((CHUNK, LANES), jnp.int32)
    for k in range(7):
        ones = ones + (lane_ids >> k & 1)
    for k in range(chunk_bits):
        ones = ones + (row_ids >> k & 1)
    inner_ones = ones.astype(jnp.float32) * (1.0 / spins)
    lane_row = bit_spin(lax.broadcasted_iota(jnp.int32, (8, LANES), 1), 0) * lane_link
    sub = lax.broadcasted_iota(jnp.int32, (CHUNK // 8, 8, LANES), 1)
    odd = (sub & 1) == 1
    second = (sub & 2) == 2
    weights = flips[...]

    def flipped(c, j):
        base = pl.multiple_of(j * CHUNK, CHUNK)
        x = own[0, c, pl.ds(base, CHUNK), :]
        coarse = x.astype(jnp.bfloat16)
        fine = (x - coarse.astype(jnp.float32)).astype(jnp.bfloat16)
        product = jnp.dot(
            jnp.concatenate([coarse, fine], axis=1), weights, preferred_element_type=jnp.float32
        )
        total = product[:, :LANES] + product[:, LANES:]
        x3 = x.reshape(CHUNK // 8, 8, LANES)
        near = jnp.where(odd, pltpu.roll(x3, 1, 1), pltpu.roll(x3, 7, 1))
        middle = jnp.where(second, pltpu.roll(x3, 2, 1), pltpu.roll(x3, 6, 1))
        far = pltpu.roll(x3, 4, 1)
        side = fields[7] * near + fields[8] * middle + fields[9] * far
        total = total + side.reshape(CHUNK, LANES)
        for k in range(3, chunk_bits):
            size = 1 << k
            parts = [
                x[(p ^ 1) * size : ((p ^ 1) + 1) * size] for p in range(CHUNK // size)
            ]
            total = total + fields[7 + k] * jnp.concatenate(parts, axis=0)
        for k in range(chunk_bits, row_bits):
            other = pl.multiple_of((j ^ (1 << (k - chunk_bits))) * CHUNK, CHUNK)
            total = total + fields[7 + k] * own[0, c, pl.ds(other, CHUNK), :]
        for b in range(high_bits):
            total = total + fields[7 + row_bits + b] * partners[b][0, c, pl.ds(base, CHUNK), :]
        return x, total

    def body(j, carry):
        norm, tilt = carry
        base = pl.multiple_of(j * CHUNK, CHUNK)
        count = jnp.int32(0)
        for k in range(row_bits - chunk_bits):
            count = count + (j >> k & 1)
        outer_ones = count.astype(jnp.float32) * (1.0 / spins) + high_ones
        top_spin = 1 - 2 * (j >> (row_bits - chunk_bits - 1) & 1)
        constant = top_spin.astype(jnp.float32) * top_link + high_energy
        real, flip_real = flipped(0, j)
        imag, flip_imag = flipped(1, j)
        shift = inner_ones + (outer_ones - magnet)
        energy = low_energy[pl.ds(base, CHUNK), :].reshape(CHUNK // 8, 8, LANES)
        energy = (energy + (lane_row + constant)[None]).reshape(CHUNK, LANES)
        keep = factor + shift * (kick_one - damp * shift)
        turn = kick_two * shift + rate * energy
        new_real = keep * real - turn * imag - rate * flip_imag
        new_imag = keep * imag + turn * real + rate * flip_real
        out[0, 0, pl.ds(base, CHUNK), :] = new_real
        out[0, 1, pl.ds(base, CHUNK), :] = new_imag
        weight = new_real * new_real + new_imag * new_imag
        tilted = weight * (inner_ones + outer_ones)
        norm = norm + jnp.sum(weight.reshape(CHUNK // 8, 8, LANES), axis=0)
        tilt = tilt + jnp.sum(tilted.reshape(CHUNK // 8, 8, LANES), axis=0)
        return norm, tilt

    zero = jnp.zeros((8, LANES), jnp.float32)
    norm, tilt = lax.fori_loop(0, rows // CHUNK, body, (zero, zero))
    sums[0, 0] = norm
    sums[0, 1] = tilt


def one_step(blocks, table, count, params, block_params, fields, flips, low_energy, high_bits, spins):
    _, _, rows, _ = blocks.shape
    shape = (1, 2, rows, LANES)
    smem = pl.BlockSpec(memory_space=pltpu.SMEM)

    def pick(slot):
        return pl.BlockSpec(shape, lambda g, t: (t[g * (1 + high_bits) + slot], 0, 0, 0))

    grid_spec = pltpu.PrefetchScalarGridSpec(
        num_scalar_prefetch=1,
        grid=(count,),
        in_specs=[
            smem,
            smem,
            smem,
            pl.BlockSpec((2 * LANES, 2 * LANES), lambda g, t: (0, 0)),
            pl.BlockSpec((rows, LANES), lambda g, t: (0, 0)),
        ]
        + [pick(slot) for slot in range(1 + high_bits)],
        out_specs=[
            pl.BlockSpec(shape, lambda g, t: (g, 0, 0, 0)),
            pl.BlockSpec((1, 2, 8, LANES), lambda g, t: (g, 0, 0, 0)),
        ],
    )
    return pl.pallas_call(
        functools.partial(step_kernel, high_bits, spins),
        grid_spec=grid_spec,
        out_shape=[
            jax.ShapeDtypeStruct((count, 2, rows, LANES), jnp.float32),
            jax.ShapeDtypeStruct((count, 2, 8, LANES), jnp.float32),
        ],
        compiler_params=pltpu.CompilerParams(vmem_limit_bytes=58 << 20),
    )(table, params, block_params, fields, flips, low_energy, *([blocks] * (1 + high_bits)))


def shards(state, fields, couplings, noise):
    local_len = state.shape[2]
    low_bits = local_len.bit_length() - 1
    blocks_all = lax.axis_size("gx")
    high_bits = blocks_all.bit_length() - 1
    spins = low_bits + high_bits
    steps = noise.shape[1]
    rows = local_len // LANES
    me = lax.axis_index("gx")
    f32 = jnp.float32

    order = sorted(range(blocks_all), key=lambda p: (bin(p).count("1"), p))
    place = {p: g for g, p in enumerate(order)}

    x = state.reshape(2, rows, LANES)
    row_ids = lax.broadcasted_iota(jnp.int32, (rows, LANES), 0)
    lane_ids = lax.broadcasted_iota(jnp.int32, (rows, LANES), 1)
    position = row_ids * LANES + lane_ids
    low_energy = jnp.zeros((rows, LANES), f32)
    occupancy = jnp.zeros((rows, LANES), jnp.int32)
    for q in range(low_bits):
        occupancy = occupancy + (position >> q & 1)
    for q in range(low_bits - 1):
        low_energy = low_energy + couplings[q] * bit_spin(position, q) * bit_spin(position, q + 1)
    own_ones = lax.population_count(me)
    weight = x[0] * x[0] + x[1] * x[1]
    start = jnp.stack(
        [
            jnp.sum(weight),
            jnp.sum(weight * ((occupancy + own_ones).astype(f32) * (1.0 / spins))),
        ]
    )
    totals = lax.psum(start, "gx")

    ids = lax.iota(jnp.int32, LANES)
    distance = ids[:, None] ^ ids[None, :]
    lane_flip = jnp.zeros((LANES, LANES), f32)
    for q in range(7):
        lane_flip = lane_flip + fields[q] * (distance == 1 << q).astype(f32)
    coarse = lax.reduce_precision(lane_flip, 8, 7)
    fine = (lane_flip - coarse).astype(jnp.bfloat16)
    coarse = coarse.astype(jnp.bfloat16)
    flips = jnp.concatenate(
        [
            jnp.concatenate([coarse, fine], axis=1),
            jnp.concatenate([coarse, jnp.zeros_like(fine)], axis=1),
        ],
        axis=0,
    )

    targets = me ^ jnp.array(order, jnp.int32)
    high_spin = [bit_spin(targets, b) for b in range(high_bits)]
    high_energy = jnp.zeros((blocks_all,), f32)
    for b in range(high_bits - 1):
        high_energy = high_energy + couplings[low_bits + b] * high_spin[b] * high_spin[b + 1]
    block_params = jnp.stack(
        [
            lax.population_count(targets).astype(f32) * (1.0 / spins),
            couplings[low_bits - 1] * high_spin[0],
            couplings[spins - 1] * high_spin[-1],
            high_energy,
        ],
        axis=1,
    ).reshape(-1)

    ring = list(range(0, blocks_all, 2)) + list(range(blocks_all - 1, 0, -2))
    ahead = [(ring[i - 1], ring[i]) for i in range(blocks_all)]
    back = [(target, source) for source, target in ahead]
    half = blocks_all // 2
    slots = [None] * blocks_all
    slots[0] = x
    from_back = from_ahead = x
    for hop in range(1, half):
        from_back = lax.ppermute(from_back, "gx", ahead)
        from_ahead = lax.ppermute(from_ahead, "gx", back)
        slots[hop] = from_back
        slots[blocks_all - hop] = from_ahead
    slots[half] = jnp.concatenate(
        [lax.ppermute(from_back[:1], "gx", ahead), lax.ppermute(from_ahead[1:], "gx", back)]
    )
    blocks = jnp.stack(slots)

    def ring_place(i):
        return jnp.where(i & 1 == 1, blocks_all - 1 - (i >> 1), i >> 1)

    half_root = jnp.sqrt(f32(time_step / 2.0))
    root_kappa = jnp.sqrt(f32(kappa_rate))
    records = []
    for s in range(steps):
        reach = steps - 1 - s
        count = sum(bin(p).count("1") <= reach for p in order)
        if blocks_all - count <= 1:
            count = blocks_all
        table = [[place[order[g]]] + [place[order[g] ^ 1 << b] for b in range(high_bits)] for g in range(count)]
        if s == 0:
            absolute = [[order[slot] for slot in entry] for entry in table]
            target = me ^ jnp.array(absolute, jnp.int32).reshape(-1)
            table = (ring_place(me) - ring_place(target)) & (blocks_all - 1)
        else:
            table = jnp.array(table, jnp.int32).reshape(-1)
        magnet = totals[1] / totals[0]
        factor = jnp.sqrt(f32(local_len * blocks_all) / totals[0])
        first = noise[0, s, 0] * half_root
        second = noise[0, s, 1] * half_root
        params = jnp.stack(
            [
                factor * time_step,
                factor,
                factor * (time_step * kappa_rate * 0.5),
                factor * root_kappa * first,
                factor * root_kappa * second,
                magnet,
            ]
        )
        drift = root_kappa * magnet * time_step
        records.append(jnp.stack([drift + first, drift + second]))
        blocks, sums = one_step(
            blocks, table, count, params, block_params, fields, flips, low_energy, high_bits, spins
        )
        if s < steps - 1:
            if count == blocks_all:
                totals = jnp.sum(sums, axis=(0, 2, 3))
            else:
                totals = lax.psum(jnp.sum(sums[0], axis=(1, 2)), "gx")
    local = jnp.where(me == 0, jnp.stack(records), 0.0)
    record = lax.psum(local, ("gx", "gy"))
    return blocks.reshape(1, 2, local_len), record


def solution(mesh):
    placed = (P("gy", None, "gx"), P(), P(), P("gy", None, None))
    return jax.shard_map(
        shards, mesh=mesh, in_specs=placed, out_specs=(P("gy", None, "gx"), P()), check_vma=False
    )
```

profile of v0, /device:TPU:1, one launch (start us, length us, event | category | flops | bytes accessed | tf_op | source)
XLA Modules:
  0.0 764.3 jit_solution(5326937247487450440)
XLA Ops:
  0.6 4.7 copy_bitcast_fusion
  7.4 90.3 %collective-permute-done = f32[2,4096,128]{2,1,0:T(8,128)} collective-permute-done((f32[2,4096,128]{2,1,0:T(8,128)S(1)}, f32[2,4096,128]{2,1,0:T(8,128)}, u32[]{:S(2)}, u32[]{:S(2)}) %collective-permute-start) | collective-permute-done | bytes 4194336 | tf_op jit(solution)/shard_map/ppermute | solution.py:214
  99.2 3.6 shift-right-arithmetic_and_fusion.4
  102.9 10.6 %fusion.29 = (f32[]{:T(128)}, f32[]{:T(128)}) fusion(s32[]{:T(128)S(6)} %population_count.6, s32[1,1,524288]{2,1,0:T(1,128)S(1)} %bitcast.122, s32[1,1,524288]{2,1,0:T(1,128)S(1)} %bitcast.123, s32[1,1,524288]{2,1,0:T(1,128)S(1)} %bitcast.124, s32[1,1,524288]{2,1,0:T(1,128)S(1)} %bitcast.125, s32[1,1,524288]{2,1,0:T(1,128)S(1)} %bitcast.126, ...), kind=kLoop, calls=%fused_computation.86 | loop fusion | flops 7340030 | bytes 16777228 | tf_op jit(solution)/shard_map/reduce_sum | solution.py:169
  114.8 85.3 %psum.21 = f32[2]{0:T(128)S(1)} all-reduce(f32[2]{0:T(128)S(1)} %pad_maximum_fusion.1), channel_id=1, replica_groups=mesh['gx'=8,'gy'=4] {'gx'}, use_global_device_ids=true, to_apply=%region_2.0 | all-reduce | flops 2 | bytes 16 | tf_op jit(solution)/shard_map/psum | solution.py:173
  202.9 2.6 fusion.14
  217.5 4.5 reduce-precision_convert_fusion
  223.2 23.3 %multiply_add_fusion.low_energy = f32[4096,128]{1,0:T(8,128)} fusion(f32[]{:T(128)} %bitcast.47, f32[]{:T(128)} %bitcast.46, f32[]{:T(128)} %bitcast.45, f32[]{:T(128)} %bitcast.44, f32[]{:T(128)} %bitcast.43, f32[]{:T(128)} %bitcast.42, f32[]{:T(128)} %bitcast.41, f32[]{:T(128)} %bitcast.40, f32[]{:T(128)} %bitcast.39, f32[]{:T(128)} %bitcast.38, ...), kind=kLoop, calls=%fused_computation.11 | loop fusion | flops 78118912 | bytes 2113608 | tf_op jit(solution)/shard_map/add | solution.py:164
  246.6 4.4 bitcast_dynamic-update-slice_fusion.6
  251.0 42.0 %collective-permute-done.2 = f32[2,4096,128]{2,1,0:T(8,128)} collective-permute-done((f32[2,4096,128]{2,1,0:T(8,128)}, f32[2,4096,128]{2,1,0:T(8,128)}, u32[]{:S(2)}, u32[]{:S(2)}) %collective-permute-start.2) | collective-permute-done | bytes 4194336 | tf_op jit(solution)/shard_map/ppermute | solution.py:214
  298.0 4.4 bitcast_dynamic-update-slice_fusion.5
  302.4 4.4 bitcast_dynamic-update-slice_fusion.4
  306.8 30.1 %collective-permute-done.3 = f32[1,4096,128]{2,1,0:T(8,128)S(1)} collective-permute-done((f32[1,4096,128]{2,1,0:T(8,128)S(1)}, f32[1,4096,128]{2,1,0:T(8,128)S(1)}, u32[]{:S(2)}, u32[]{:S(2)}) %collective-permute-start.3) | collective-permute-done | bytes 2097184 | tf_op jit(solution)/shard_map/ppermute | solution.py:219
  337.6 2.2 fusion
  339.8 4.4 bitcast_dynamic-update-slice_fusion.3
  344.2 4.4 bitcast_dynamic-update-slice_fusion.2
  348.7 4.4 bitcast_dynamic-update-slice_fusion.1.own.rest_0_.rest_1_.rest_2_
  353.0 119.1 %shard_map.104 = (f32[8,2,4096,128]{3,2,1,0:T(8,128)}, f32[8,2,8,128]{3,2,1,0:T(8,128)}) custom-call(s32[32]{0:T(128)} %fusion.28.table, f32[6]{0:T(128)} %stack.174.params, f32[32]{0:T(128)} %reshape.346.block_params, f32[22]{0:T(128)} %fields.7, bf16[256,256]{1,0:T(8,128)(2,1)} %fusion.2.flips, f32[4096,128]{1,0:T(8,128)} %multiply_add_fusion.low_energy, ...), custom_call_target="tpu_custom_call" | custom-call | tf_op jit(solution)/shard_map/pallas_call | solution.py:130
  477.4 119.0 %shard_map.105 = (f32[8,2,4096,128]{3,2,1,0:T(8,128)}, f32[8,2,8,128]{3,2,1,0:T(8,128)}) custom-call(s32[32]{0:T(128)} %constant.135.table, f32[6]{0:T(128)} %stack.192.params, f32[32]{0:T(128)} %reshape.346.block_params, f32[22]{0:T(128)} %fields.7, bf16[256,256]{1,0:T(8,128)(2,1)} %fusion.2.flips, f32[4096,128]{1,0:T(8,128)} %multiply_add_fusion.low_energy, ...), custom_call_target="tpu_custom_call" | custom-call | tf_op jit(solution)/shard_map/pallas_call | solution.py:130
  601.9 64.7 %shard_map.106 = (f32[4,2,4096,128]{3,2,1,0:T(8,128)}, f32[4,2,8,128]{3,2,1,0:T(8,128)}) custom-call(s32[16]{0:T(128)} %constant.134.table, f32[6]{0:T(128)} %stack.197.params, f32[32]{0:T(128)} %reshape.346.block_params, f32[22]{0:T(128)} %fields.7, bf16[256,256]{1,0:T(8,128)(2,1)} %fusion.2.flips, f32[4096,128]{1,0:T(8,128)} %multiply_add_fusion.low_energy, ...), custom_call_target="tpu_custom_call" | custom-call | tf_op jit(solution)/shard_map/pallas_call | solution.py:130
  667.3 14.6 %psum.22 = f32[2]{0:T(128)S(1)} all-reduce(f32[2]{0:T(128)S(1)} %slice_reduce_fusion), channel_id=1, replica_groups=mesh['gx'=8,'gy'=4] {'gx'}, use_global_device_ids=true, to_apply=%region_6.7 | all-reduce | flops 2 | bytes 16 | tf_op jit(solution)/shard_map/psum | solution.py:264
  686.1 46.9 %psum.23 = f32[4,2]{1,0:T(4,128)S(1)} all-reduce(f32[4,2]{1,0:T(4,128)S(1)} %maximum_select_fusion), channel_id=1, replica_groups=mesh['gx'=8,'gy'=4] {'gx','gy'}, use_global_device_ids=true, to_apply=%region_7.8 | all-reduce | flops 8 | bytes 64 | tf_op jit(solution)/shard_map/psum | solution.py:266
  734.8 22.6 %shard_map.107 = (f32[1,2,4096,128]{3,2,1,0:T(8,128)}, f32[1,2,8,128]{3,2,1,0:T(8,128)}) custom-call(s32[4]{0:T(128)} %iota.239.table, f32[6]{0:T(128)} %stack.202.params, f32[32]{0:T(128)} %reshape.346.block_params, f32[22]{0:T(128)} %fields.7, bf16[256,256]{1,0:T(8,128)(2,1)} %fusion.2.flips, f32[4096,128]{1,0:T(8,128)} %multiply_add_fusion.low_energy, ...), custom_call_target="tpu_custom_call" | custom-call | tf_op jit(solution)/shard_map/pallas_call | solution.py:130
  757.4 6.9 reshape.348
  (60 shorter events, 26.0 us)
Async XLA Ops:
  5.3 92.4 %collective-permute-start = (f32[2,4096,128]{2,1,0:T(8,128)S(1)}, f32[2,4096,128]{2,1,0:T(8,128)}, u32[]{:S(2)}, u32[]{:S(2)}) collective-permute-start(f32[2,4096,128]{2,1,0:T(8,128)S(1)} %get-tuple-element.22), channel_id=1, source_target_pairs={{4,0},{0,8},{8,16},{16,24},{24,28},{28,20},{20,12},{12,4},{5,1},{1... | collective-permute-start | bytes 12582920 | tf_op jit(solution)/shard_map/ppermute | solution.py:214
  7.4 91.6 %collective-permute-start.4 = (f32[2,4096,128]{2,1,0:T(8,128)S(1)}, f32[2,4096,128]{2,1,0:T(8,128)}, u32[]{:S(2)}, u32[]{:S(2)}) collective-permute-start(f32[2,4096,128]{2,1,0:T(8,128)S(1)} %get-tuple-element.22), channel_id=1, source_target_pairs={{0,4},{8,0},{16,8},{24,16},{28,24},{20,28},{12,20},{4,12},{1,5},{9... | collective-permute-start | bytes 12582920 | tf_op jit(solution)/shard_map/ppermute | solution.py:215
  97.7 107.7 %collective-permute-start.1 = (f32[2,4096,128]{2,1,0:T(8,128)}, f32[2,4096,128]{2,1,0:T(8,128)}, u32[]{:S(2)}, u32[]{:S(2)}) collective-permute-start(f32[2,4096,128]{2,1,0:T(8,128)} %collective-permute-done), channel_id=1, source_target_pairs={{4,0},{0,8},{8,16},{16,24},{24,28},{28,20},{20,12},{12,4},{5,1},{1... | collective-permute-start | bytes 12582920 | tf_op jit(solution)/shard_map/ppermute | solution.py:214
  99.0 106.6 %collective-permute-start.5 = (f32[2,4096,128]{2,1,0:T(8,128)}, f32[2,4096,128]{2,1,0:T(8,128)}, u32[]{:S(2)}, u32[]{:S(2)}) collective-permute-start(f32[2,4096,128]{2,1,0:T(8,128)} %collective-permute-done.4), channel_id=1, source_target_pairs={{0,4},{8,0},{16,8},{24,16},{28,24},{20,28},{12,20},{4,12},{1,5},{9... | collective-permute-start | bytes 12582920 | tf_op jit(solution)/shard_map/ppermute | solution.py:215
  99.2 3.6 copy-start
  102.8 98.7 %copy-start.1 = (f32[22]{0:T(128)S(1)}, f32[22]{0:T(128)}, u32[]{:S(2)}) copy-start(f32[22]{0:T(128)} %param.11) | copy-start | bytes 268
  102.8 100.1 %copy-start.5 = (s32[8]{0:T(128)S(1)}, s32[8]{0:T(128)}, u32[]{:S(2)}) copy-start(s32[8]{0:T(128)} %constant.124.clone) | copy-start | bytes 100
  102.9 104.1 %copy-start.4 = (f32[1,4,2]{1,2,0:T(2,128)S(1)}, f32[1,4,2]{1,2,0:T(2,128)}, u32[]{:S(2)}) copy-start(f32[1,4,2]{1,2,0:T(2,128)} %param.12) | copy-start | bytes 100
  102.9 109.2 %copy-start.3 = (s32[8,4]{1,0:T(8,128)S(1)}, s32[8,4]{1,0:T(8,128)}, u32[]{:S(2)}) copy-start(s32[8,4]{1,0:T(8,128)} %constant.125.clone) | copy-start | bytes 388
  102.9 114.0 %copy-start.2 = (f32[22]{0:T(128)S(1)}, f32[22]{0:T(128)}, u32[]{:S(2)}) copy-start(f32[22]{0:T(128)} %fields.7) | copy-start | bytes 268
  205.5 87.5 %collective-permute-start.2 = (f32[2,4096,128]{2,1,0:T(8,128)}, f32[2,4096,128]{2,1,0:T(8,128)}, u32[]{:S(2)}, u32[]{:S(2)}) collective-permute-start(f32[2,4096,128]{2,1,0:T(8,128)} %collective-permute-done.1), channel_id=1, source_target_pairs={{4,0},{0,8},{8,16},{16,24},{24,28},{28,20},{20,12},{12,4},{5,1},{1... | collective-permute-start | bytes 12582920 | tf_op jit(solution)/shard_map/ppermute | solution.py:214
  205.6 89.5 %collective-permute-start.6 = (f32[2,4096,128]{2,1,0:T(8,128)}, f32[2,4096,128]{2,1,0:T(8,128)}, u32[]{:S(2)}, u32[]{:S(2)}) collective-permute-start(f32[2,4096,128]{2,1,0:T(8,128)} %collective-permute-done.5), channel_id=1, source_target_pairs={{0,4},{8,0},{16,8},{24,16},{28,24},{20,28},{12,20},{4,12},{1,5},{9... | collective-permute-start | bytes 12582920 | tf_op jit(solution)/shard_map/ppermute | solution.py:215
  294.7 42.3 %collective-permute-start.3 = (f32[1,4096,128]{2,1,0:T(8,128)S(1)}, f32[1,4096,128]{2,1,0:T(8,128)S(1)}, u32[]{:S(2)}, u32[]{:S(2)}) collective-permute-start(f32[1,4096,128]{2,1,0:T(8,128)S(1)} %slice.208), channel_id=1, source_target_pairs={{4,0},{0,8},{8,16},{16,24},{24,28},{28,20},{20,12},{12,4},{5,1},{1... | collective-permute-start | bytes 6291464 | tf_op jit(solution)/shard_map/ppermute | solution.py:219
  296.8 40.8 %collective-permute-start.7 = (f32[1,4096,128]{2,1,0:T(8,128)S(1)}, f32[1,4096,128]{2,1,0:T(8,128)S(1)}, u32[]{:S(2)}, u32[]{:S(2)}) collective-permute-start(f32[1,4096,128]{2,1,0:T(8,128)S(1)} %slice.209), channel_id=1, source_target_pairs={{0,4},{8,0},{16,8},{24,16},{28,24},{20,28},{12,20},{4,12},{1,5},{9... | collective-permute-start | bytes 6291464 | tf_op jit(solution)/shard_map/ppermute | solution.py:219
where the time goes:
time: 768 us; the launch traced here: 764 us
  Pallas kernels  325 us (42%)
  waiting for transfers between devices  163 us (21%)
  blocking collectives  147 us (19%)
  other arithmetic  52.4 us (7%)
  local copies, waits for them, and re-layouts  51.2 us (7%)
  between operations  18.9 us (2%)
    pallas_call x4, Pallas kernels, one_step(): pl.pallas_call(functools.partial(step_kernel, high_bits, spins), grid_spe...  325 us
    ppermute x3, waiting for transfers between devices, shards(): from_back = lax.ppermute(from_back, 'gx', ahead)  132 us
    psum x1, blocking collectives, shards(): totals = lax.psum(start, 'gx')  85.3 us
    psum x1, blocking collectives, shards(): record = lax.psum(local, ('gx', 'gy'))  46.9 us
    ppermute x1, waiting for transfers between devices, shards(): lax.ppermute(from_back[:1], 'gx', ahead)  30.1 us
    add x1, other arithmetic, shards(): low_energy + couplings[q] * bit_spin(position, q) * bit_spin(position, q...  23.3 us
    unnamed x18, local copies, waits for them, and re-layouts  22.8 us
  transfers between devices with their start and end apart: 8, of which 4 were waited for; matrix products, arithmetic and copies ran while one was open for 9% of the time, Pallas kernels for 0%

commit v1 on v0

v1 whole, which is shorter than its diff:
```python
import functools

import jax
import jax.numpy as jnp
from jax import lax
from jax.experimental import pallas as pl
from jax.experimental.pallas import tpu as pltpu
from jax.sharding import PartitionSpec as P

KAPPA = 4.0
DT = 0.05
LANES = 128
LANE_BITS = 7
CHUNK = 128
PIECES = 8
MESH = pl.DeviceIdType.MESH


def ones_in(value):
    return bin(value).count("1")


def bit_of(value, k):
    return lax.rem(lax.div(value, 1 << k), 2)


def flip_bit(value, k):
    return value + (1 - 2 * bit_of(value, k)) * (1 << k)


def flip_bits(value, mask):
    k = 0
    while mask >> k:
        if mask >> k & 1:
            value = flip_bit(value, k)
        k += 1
    return value


def spin(bit):
    return (1 - 2 * bit).astype(jnp.float32)


def wait_bytes(ref, sem):
    pltpu.make_async_copy(ref, ref, sem).wait()


def evolve_kernel(
    bits, paths, steps, spins,
    fields, couplings, noise, state, out, record,
    buf, far, weights, table, outer_energy, outer_ones, edge, sums, marks, kicks,
    own_sem, swap_send, noise_sem, noise_send, arrive, push_send, relay_send,
    far_send, far_recv, sum_send, sum_recv, mark_send, mark_recv, out_sem, out_send, free,
):
    f32 = jnp.float32
    blocks = 1 << bits
    rows = state.shape[0]
    row_bits = rows.bit_length() - 1
    chunk_bits = CHUNK.bit_length() - 1
    chunks = rows // CHUNK
    piece = rows // PIECES
    piece_chunks = piece // CHUNK
    groups = CHUNK // 8

    gx, gy = lax.axis_index("gx"), lax.axis_index("gy")
    high, low = lax.div(gx, blocks), lax.rem(gx, blocks)
    path, core = lax.div(gy, 2), lax.rem(gy, 2)
    home = high == core
    away = high != core
    swap_device = {"gx": core * blocks + low, "gy": path * 2 + high}
    core_device = {"gx": gx, "gy": path * 2 + 1 - core}

    def bit_device(b):
        return {"gx": high * blocks + flip_bit(low, b), "gy": gy}

    def sum_device(o):
        c = 1 - core if o >> bits & 1 else core
        return {"gx": high * blocks + flip_bits(low, o % blocks), "gy": path * 2 + c}

    def mark_device(o):
        h = 1 - high if o & 1 else high
        return {"gx": h * blocks + low, "gy": lax.rem(path + (o >> 1), paths) * 2 + core}

    def remote(src, dst, send, recv, device):
        return pltpu.make_async_remote_copy(
            src_ref=src, dst_ref=dst, send_sem=send, recv_sem=recv, device_id=device, device_id_type=MESH
        )

    def rows_of(p):
        return pl.ds(p * piece, piece)

    @pl.when(home)
    def _():
        for p in range(PIECES):
            pltpu.make_async_copy(state.at[rows_of(p)], buf.at[0, 0, rows_of(p)], own_sem.at[p]).start()
        pltpu.make_async_copy(noise, kicks, noise_sem).start()

    @pl.when(away)
    def _():
        remote(noise, kicks, noise_send, noise_sem, swap_device).start()
        for p in range(PIECES):
            remote(
                state.at[rows_of(p)], buf.at[0, 0, rows_of(p)], swap_send, own_sem.at[p], swap_device
            ).start()

    lane_a = lax.broadcasted_iota(jnp.int32, (LANES, LANES), 0)
    lane_b = lax.broadcasted_iota(jnp.int32, (LANES, LANES), 1)
    distance = lane_a ^ lane_b
    lane_flip = jnp.zeros((LANES, LANES), f32)
    for q in range(LANE_BITS):
        lane_flip = jnp.where(distance == 1 << q, fields[q], lane_flip)
    coarse_flip = lane_flip.astype(jnp.bfloat16)
    fine_flip = (lane_flip - coarse_flip.astype(f32)).astype(jnp.bfloat16)
    weights[:LANES, :LANES] = coarse_flip
    weights[:LANES, LANES:] = fine_flip
    weights[LANES:, :LANES] = coarse_flip
    weights[LANES:, LANES:] = jnp.zeros_like(fine_flip)

    row_ids = lax.broadcasted_iota(jnp.int32, (CHUNK, LANES), 0)
    lane_ids = lax.broadcasted_iota(jnp.int32, (CHUNK, LANES), 1)
    inner_bits = [lane_ids >> q & 1 for q in range(LANE_BITS)]
    inner_bits += [row_ids >> k & 1 for k in range(1, chunk_bits)]
    inner_count = len(inner_bits)
    inner_energy = jnp.zeros((CHUNK, LANES), f32)
    inner_ones = jnp.zeros((CHUNK, LANES), jnp.int32)
    for q in range(inner_count):
        inner_ones = inner_ones + inner_bits[q]
        if q + 1 < inner_count:
            inner_energy = inner_energy + couplings[q] * (spin(inner_bits[q]) * spin(inner_bits[q + 1]))
    table[0] = inner_energy
    table[1] = inner_ones.astype(f32) * (1.0 / spins)

    chunk_qubits = row_bits - chunk_bits
    top_spin = spin(core)
    low_spins = [spin(bit_of(low, b)) for b in range(bits)]

    def fill(k, carry):
        ids = [bit_of(k, t) for t in range(chunk_qubits)]
        z = [spin(b) for b in ids]
        count = ids[0]
        for b in ids[1:]:
            count = count + b
        energy = f32(0.0)
        for t in range(chunk_qubits - 1):
            energy = energy + couplings[inner_count + t] * (z[t] * z[t + 1])
        edge[k] = couplings[inner_count - 1] * z[0]
        for j in range(blocks):
            zb = [low_spins[b] * (-1.0 if j >> b & 1 else 1.0) for b in range(bits)] + [top_spin]
            ones_j = count + core
            for b in range(bits):
                ones_j = ones_j + (1 - bit_of(low, b) if j >> b & 1 else bit_of(low, b))
            e = energy + couplings[spins - 2 - bits] * (z[-1] * zb[0])
            for b in range(bits):
                e = e + couplings[spins - 1 - bits + b] * (zb[b] * zb[b + 1])
            outer_energy[j * chunks + k] = e
            outer_ones[j * chunks + k] = ones_j.astype(f32) * (1.0 / spins)
        return carry

    lax.fori_loop(0, chunks, fill, 0)

    sub = lax.broadcasted_iota(jnp.int32, (8, LANES), 0)
    imag = (sub & 1) == 1
    upper = (sub & 2) == 2
    lane_edge = spin(lax.broadcasted_iota(jnp.int32, (8, LANES), 1) & 1) * (couplings[spins - 1] * top_spin)

    def start_sums(s, norm, tilt):
        sums[s, 0, :8] = norm
        sums[s, 0, 8:] = tilt
        for o in range(1, 2 * blocks):
            remote(
                sums.at[s, 0], sums.at[s, o], sum_send.at[s], sum_recv.at[s], sum_device(o)
            ).start()

    def finish_sums(s):
        others = sums.at[s, pl.ds(1, 2 * blocks - 1)]
        wait_bytes(others, sum_recv.at[s])
        wait_bytes(others, sum_send.at[s])
        total = sums[s, 0]
        for o in range(1, 2 * blocks):
            total = total + sums[s, o]
        norm = jnp.full((8, LANES), jnp.sum(total[:8]), f32)
        tilt = jnp.full((8, LANES), jnp.sum(total[8:]), f32)
        return norm, tilt

    zero = jnp.zeros((8, LANES), f32)

    def first_sums():
        def body(k, carry):
            norm, tilt = carry
            x = buf[0, 0, pl.ds(pl.multiple_of(k * CHUNK, CHUNK), CHUNK), :]
            w = x * x
            ones = table[1] + outer_ones[k]
            norm = norm + jnp.sum(w.reshape(groups, 8, LANES), axis=0)
            tilt = tilt + jnp.sum((w * ones).reshape(groups, 8, LANES), axis=0)
            return norm, tilt

        return lax.fori_loop(0, chunks, body, (zero, zero))

    def step_values(s):
        norm, tilt = finish_sums(s)
        magnet = tilt / norm
        factor = jnp.sqrt(f32(rows * (LANES // 2) * 2 * blocks) / norm)
        half_root = jnp.sqrt(jnp.full((8, LANES), DT / 2.0, f32))
        root_kappa = jnp.sqrt(jnp.full((8, LANES), KAPPA, f32))
        first = kicks[pl.ds(2 * s, 1), :] * half_root
        second = kicks[pl.ds(2 * s + 1, 1), :] * half_root
        drift = root_kappa * magnet * DT
        marks[0, pl.ds(2 * s, 1), :] = (drift + first)[:1]
        marks[0, pl.ds(2 * s + 1, 1), :] = (drift + second)[:1]
        ratio = root_kappa * second * (1.0 / DT)
        damp = factor * (DT * KAPPA * 0.5)
        inner = table[1].reshape(groups, 8, LANES)
        table[2] = (table[0].reshape(groups, 8, LANES) + ratio * inner).reshape(CHUNK, LANES)
        table[3] = (-(damp * inner) * inner).reshape(CHUNK, LANES)
        rate = factor * DT
        return dict(
            magnet=magnet, factor=factor, kick=factor * root_kappa * first, damp=damp, ratio=ratio,
            rate=jnp.where(imag, -rate, rate),
        )

    def update(src, j, begin, end, values, sums_too, carry=None):
        dst = 1 - src

        def body(k, carry):
            base = pl.multiple_of(k * CHUNK, CHUNK)
            here = pl.ds(base, CHUNK)
            x = buf[src, j, here, :]
            coarse = x.astype(jnp.bfloat16)
            fine = (x - coarse.astype(f32)).astype(jnp.bfloat16)
            product = jnp.dot(
                jnp.concatenate([coarse, fine], axis=1), weights[...], preferred_element_type=f32
            )
            total = product[:, :LANES] + product[:, LANES:]
            x3 = x.reshape(groups, 8, LANES)
            near = jnp.where(upper[None], pltpu.roll(x3, 2, 1), pltpu.roll(x3, 6, 1))
            total = total.reshape(groups, 8, LANES) + fields[7] * near + fields[8] * pltpu.roll(x3, 4, 1)
            for t in range(3, chunk_bits):
                size = 1 << (t - 3)
                parts = [x3[(i ^ 1) * size : ((i ^ 1) + 1) * size] for i in range(groups // size)]
                total = total + fields[6 + t] * jnp.concatenate(parts, axis=0)
            for t in range(chunk_bits, row_bits):
                other = pl.multiple_of(flip_bit(k, t - chunk_bits) * CHUNK, CHUNK)
                total = total + fields[6 + t] * buf[src, j, pl.ds(other, CHUNK), :].reshape(groups, 8, LANES)
            for b in range(bits):
                total = total + fields[6 + row_bits + b] * buf[src, j ^ 1 << b, here, :].reshape(groups, 8, LANES)
            total = total + fields[spins - 1] * far[j, here, :].reshape(groups, 8, LANES)

            ones = outer_ones[j * chunks + k]
            shift = ones - values["magnet"]
            constant = values["factor"] + shift * (values["kick"] - values["damp"] * shift)
            slope = values["kick"] - 2.0 * (values["damp"] * shift)
            level = lane_edge + outer_energy[j * chunks + k] + values["ratio"] * shift
            inner = table[1].reshape(groups, 8, LANES)
            side = jnp.concatenate(
                [jnp.broadcast_to((level + edge[k])[None], (groups // 2, 8, LANES)),
                 jnp.broadcast_to((level - edge[k])[None], (groups // 2, 8, LANES))], axis=0
            )
            diagonal = table[2].reshape(groups, 8, LANES) + side
            turned = values["rate"] * (total + x3 * diagonal)
            turned = jnp.where(imag[None], pltpu.roll(turned, 1, 1), pltpu.roll(turned, 7, 1))
            keep = table[3].reshape(groups, 8, LANES) + constant + slope * inner
            new = keep * x3 + turned
            buf[dst, j, here, :] = new.reshape(CHUNK, LANES)
            if not sums_too:
                return carry
            norm, tilt = carry
            w = new * new
            some = jnp.sum(w, axis=0)
            return norm + some, tilt + jnp.sum(w * inner, axis=0) + ones * some

        if not sums_too:
            lax.fori_loop(begin, end, body, 0)
            return None
        return lax.fori_loop(begin, end, body, carry or (zero, zero))

    def send_far(src, j, where=None):
        where = pl.ds(0, rows) if where is None else where
        remote(
            buf.at[src, j, where], far.at[j, where], far_send.at[j], far_recv.at[j], core_device
        ).start()

    order = sorted(range(blocks), key=lambda j: (ones_in(j), j))
    levels = [[j for j in order if ones_in(j) == n] for n in range(bits + 1)]

    def last_hop(j, p):
        on = [b for b in range(bits) if j >> b & 1]
        return on[-1] if p % 4 == 3 else on[(p // 4) % (len(on) - 1)]

    def arrived(j, p):
        wait_bytes(buf.at[0, j, rows_of(p)], arrive.at[j, p])
        send_far(0, j, rows_of(p))
        for b in range(bits):
            target = j | 1 << b
            if not j >> b & 1 and last_hop(target, p) == b:
                remote(
                    buf.at[0, j, rows_of(p)], buf.at[0, target, rows_of(p)],
                    relay_send.at[target], arrive.at[target, p], bit_device(b),
                ).start()

    lag = 2
    for p in range(PIECES):
        wait_bytes(buf.at[0, 0, rows_of(p)], own_sem.at[p])
        for b in range(bits):
            remote(
                buf.at[0, 0, rows_of(p)], buf.at[0, 1 << b, rows_of(p)],
                push_send.at[b], arrive.at[1 << b, p], bit_device(b),
            ).start()
        send_far(0, 0, rows_of(p))
        if p >= lag:
            for j in levels[1]:
                arrived(j, p - lag)
    start_sums(0, *first_sums())
    for p in range(PIECES - lag, PIECES):
        for j in levels[1]:
            arrived(j, p)
    wait_bytes(kicks, noise_sem)

    values = step_values(0)
    everything = pl.ds(0, rows)

    def far_ready(j):
        wait_bytes(far.at[j, everything], far_recv.at[j])

    def whole(src, j, sums_too):
        far_ready(j)
        return update(src, j, 0, chunks, values, sums_too)

    sums_next = None
    for n in range(2, bits + 1):
        for j in levels[n - 2]:
            got = whole(0, j, j == 0)
            if j == 0:
                start_sums(1, *got)
        if n < bits:
            for p in range(PIECES):
                for j in levels[n]:
                    arrived(j, p)
    for j in levels[bits - 1]:
        far_ready(j)
    got = (zero, zero)
    last = levels[bits][0]
    for p in range(PIECES):
        arrived(last, p)
        for j in levels[bits - 1]:
            part = update(0, j, p * piece_chunks, (p + 1) * piece_chunks, values, j == 0, got)
            if j == 0:
                got = part
    if bits == 1:
        start_sums(1, *got)
    whole(0, last, False)

    @pl.when(away)
    def _():
        wait_bytes(state, swap_send)
        wait_bytes(noise, noise_send)

    for b in range(bits):
        wait_bytes(buf.at[0, 0], push_send.at[b])
    for j in order:
        if ones_in(j) >= 2:
            wait_bytes(buf.at[0, j], relay_send.at[j])

    in_flight = set(order)

    def send_next(src, j):
        pl.semaphore_wait(free.at[j], 1)
        wait_bytes(buf.at[src, j], far_send.at[j])
        send_far(src, j)

    def needed(s):
        return [j for j in order if ones_in(j) <= steps - 1 - s]

    for j in needed(1):
        pl.semaphore_signal(free.at[j], 1, device_id=core_device, device_id_type=MESH)
    for j in needed(1):
        send_next(1, j)

    for s in range(1, steps - 1):
        src = s % 2
        values = step_values(s)
        waiting = None
        for j in needed(s):
            got = whole(src, j, j == 0)
            if j == 0:
                start_sums(s + 1, *got)
            if j in needed(s + 1):
                pl.semaphore_signal(free.at[j], 1, device_id=core_device, device_id_type=MESH)
            if waiting is not None:
                send_next(1 - src, waiting)
            waiting = j if j in needed(s + 1) else None
        if waiting is not None:
            send_next(1 - src, waiting)

    src = (steps - 1) % 2
    values = step_values(steps - 1)
    for o in range(1, 2 * paths):
        remote(marks.at[0], marks.at[o], mark_send, mark_recv, mark_device(o)).start()
    far_ready(0)

    def deliver(p):
        @pl.when(home)
        def _():
            pltpu.make_async_copy(buf.at[1 - src, 0, rows_of(p)], out.at[rows_of(p)], out_sem).start()

        @pl.when(away)
        def _():
            remote(
                buf.at[1 - src, 0, rows_of(p)], out.at[rows_of(p)], out_send, out_sem, swap_device
            ).start()

    for p in range(PIECES):
        update(src, 0, p * piece_chunks, (p + 1) * piece_chunks, values, False)
        if p:
            deliver(p - 1)
    deliver(PIECES - 1)

    others = marks.at[pl.ds(1, 2 * paths - 1)]
    wait_bytes(others, mark_recv)
    wait_bytes(others, mark_send)
    total = marks[0]
    for o in range(1, 2 * paths):
        total = total + marks[o]
    record[...] = total
    for j in order:
        wait_bytes(buf.at[0, j], far_send.at[j])
    wait_bytes(out, out_sem)

    @pl.when(away)
    def _():
        wait_bytes(out, out_send)


def shards(state, fields, couplings, noise):
    local_len = state.shape[2]
    steps = noise.shape[1]
    bits = lax.axis_size("gx").bit_length() - 2
    paths = lax.axis_size("gy") // 2
    spins = local_len.bit_length() - 1 + bits + 1
    blocks = 1 << bits
    rows = 2 * local_len // LANES
    chunks = rows // CHUNK
    f32 = jnp.float32
    mixed = state.reshape(2, rows // 2, LANES).transpose(1, 0, 2).reshape(rows, LANES)
    kicks = jnp.broadcast_to(noise.reshape(steps * 2, 1), (steps * 2, LANES))
    smem = pl.BlockSpec(memory_space=pltpu.SMEM)
    hbm = pl.BlockSpec(memory_space=pl.ANY)
    dma, regular = pltpu.SemaphoreType.DMA, pltpu.SemaphoreType.REGULAR
    tile = (steps * 2, LANES)
    out, record = pl.pallas_call(
        functools.partial(evolve_kernel, bits, paths, steps, spins),
        in_specs=[smem, smem, hbm, hbm],
        out_specs=[hbm, pl.BlockSpec(memory_space=pltpu.VMEM)],
        out_shape=[jax.ShapeDtypeStruct((rows, LANES), f32), jax.ShapeDtypeStruct(tile, f32)],
        scratch_shapes=[
            pltpu.VMEM((2, blocks, rows, LANES), f32),
            pltpu.VMEM((blocks, rows, LANES), f32),
            pltpu.VMEM((2 * LANES, 2 * LANES), jnp.bfloat16),
            pltpu.VMEM((4, CHUNK, LANES), f32),
            pltpu.SMEM((blocks * chunks,), f32),
            pltpu.SMEM((blocks * chunks,), f32),
            pltpu.SMEM((chunks,), f32),
            pltpu.VMEM((steps, 2 * blocks, 16, LANES), f32),
            pltpu.VMEM((2 * paths,) + tile, f32),
            pltpu.VMEM(tile, f32),
            dma((PIECES,)), dma, dma, dma, dma((blocks, PIECES)), dma((bits,)), dma((blocks,)),
            dma((blocks,)), dma((blocks,)), dma((steps,)), dma((steps,)), dma, dma, dma, dma,
            regular((blocks,)),
        ],
        compiler_params=pltpu.CompilerParams(has_side_effects=True, vmem_limit_bytes=60 << 20),
    )(fields, couplings, kicks, mixed)
    final = out.reshape(rows // 2, 2, LANES).transpose(1, 0, 2).reshape(1, 2, local_len)
    return final, record[:, 0].reshape(steps, 2)


def solution(mesh):
    placed = (P("gy", None, "gx"), P(), P(), P("gy", None, None))
    return jax.shard_map(
        shards, mesh=mesh, in_specs=placed, out_specs=(P("gy", None, "gx"), P()), check_vma=False
    )
```

time: 768 us -> 434 us (0.57)
  waiting for transfers between devices: 163 us -> 0 us
  blocking collectives: 147 us -> 0 us
  Pallas kernels: 325 us -> 425 us
  other arithmetic: 52.4 us -> 0 us
  local copies, waits for them, and re-layouts: 51.2 us -> 7.78 us
  between operations: 18.9 us -> 0.64 us
    ppermute x8 -> x0, waiting for transfers between devices: 163 us -> none  [the longest x3 132 us: shards(): from_back = lax.ppermute(from_back, 'gx', ahead)]
    psum x3 -> x0, blocking collectives: 147 us -> none  [the longest x1 85.3 us: shards(): totals = lax.psum(start, 'gx')]
    pallas_call x4 -> x1, Pallas kernels: 325 us -> 425 us  [shards(): pl.pallas_call(functools.partial(evolve_kernel, bits, paths, steps, spins...]
    add x1 -> x0, other arithmetic: 23.3 us -> none  [shards(): low_energy + couplings[q] * bit_spin(position, q) * bit_spin(position, q...]
    unnamed x18 -> x3, local copies, waits for them, and re-layouts: 22.8 us -> 6.14 us
    reduce_sum x4 -> x0, other arithmetic: 13.3 us -> none  [the longest x1 10.6 us: shards(): jnp.sum(weight)]
    reshape x4 -> x0, local copies, waits for them, and re-layouts: 12.6 us -> none  [the longest x1 6.87 us: shards(): return (blocks.reshape(1, 2, local_len), record)]
    slice x10 -> x1, local copies, waits for them, and re-layouts: 8.5 us -> 0.8 us  [shards(): return (final, record[:, 0].reshape(steps, 2))]
  transfers between devices with their start and end apart: 8 -> 0, of which waited for: 4 -> 0; matrix products, arithmetic and copies ran while one was open for 9% -> 0% of each run, Pallas kernels for 0% -> 0%
where the time goes in v1:
time: 434 us
  Pallas kernels  425 us (98%)
  local copies, waits for them, and re-layouts  7.78 us (2%)
    pallas_call x1, Pallas kernels, shards(): pl.pallas_call(functools.partial(evolve_kernel, bits, paths, steps, spins...  425 us

profile of v1, /device:TPU:1, one launch (start us, length us, event | category | flops | bytes accessed | tf_op | source)
XLA Modules:
  0.0 433.9 jit_solution(6350633218964789222)
XLA Ops:
  0.6 0.8 copy.10
  1.4 0.1 broadcast_in_dim.7
  1.5 0.7 broadcast_in_dim.8.noise
  2.1 425.5 %shard_map.59 = (f32[8192,128]{1,0:T(8,128)}, f32[8,128]{1,0:T(8,128)}) custom-call(f32[22]{0:T(128)} %fields.1, f32[22]{0:T(128)} %couplings.1, f32[8,128]{1,0:T(8,128)} %broadcast_in_dim.8.noise, f32[8192,128]{1,0:T(8,128)} %bitcast.10), custom_call_target="tpu_custom_call" | custom-call | tf_op jit(solution)/shard_map/pallas_call | solution.py:449
  427.6 0.8 slice_reduce_fusion
  428.4 0.1 reshape_squeeze.3
  428.5 0.7 copy.13
  429.2 4.7 %copy.15 = f32[1,2,524288]{2,1,0:T(2,128)} copy(f32[1,2,524288]{2,1,0:T(2,128)} %bitcast.11) | data formatting | bytes 8388608

commit v2 on v1

v2 whole, which is shorter than its diff:
```python
import functools

import jax
import jax.numpy as jnp
from jax import lax
from jax.experimental import pallas as pl
from jax.experimental.pallas import tpu as pltpu
from jax.sharding import PartitionSpec as P

KAPPA = 4.0
DT = 0.05
LANES = 128
LANE_BITS = 7
SIDE = 256
SIDE_BITS = 8
CHUNK = 2 * SIDE
PART = 64
PIECES = 8
MESH = pl.DeviceIdType.MESH


def ones_in(value):
    return bin(value).count("1")


def bit_of(value, k):
    return lax.rem(lax.div(value, 1 << k), 2)


def flip_bit(value, k):
    return value + (1 - 2 * bit_of(value, k)) * (1 << k)


def flip_bits(value, mask):
    k = 0
    while mask >> k:
        if mask >> k & 1:
            value = flip_bit(value, k)
        k += 1
    return value


def other_block(j, b):
    return j ^ 1 << b if isinstance(j, int) else flip_bit(j, b)


def spin(bit):
    return (1 - 2 * bit).astype(jnp.float32)


def wait_bytes(ref, sem):
    pltpu.make_async_copy(ref, ref, sem).wait()


def evolve_kernel(
    bits, paths, steps, spins,
    fields, couplings, noise, state, out, record,
    even, odd, far, row_flips, pair_flips, ahead, later, table, outer_energy, outer_ones, edge, sums, marks, kicks,
    own_sem, swap_send, noise_sem, noise_send, arrive, push_send, relay_send,
    far_send, far_recv, sum_send, sum_recv, mark_send, mark_recv, out_sem, out_send, free,
):
    f32 = jnp.float32
    blocks = 1 << bits
    rows = state.shape[0]
    row_bits = rows.bit_length() - 1
    chunk_bits = CHUNK.bit_length() - 1
    bufs = (even, odd)
    chunks = rows // CHUNK
    piece = rows // PIECES
    piece_chunks = piece // CHUNK
    groups = SIDE // 8
    part_groups = PART // 8

    gx, gy = lax.axis_index("gx"), lax.axis_index("gy")
    high, low = lax.div(gx, blocks), lax.rem(gx, blocks)
    path, core = lax.div(gy, 2), lax.rem(gy, 2)
    home = high == core
    away = high != core
    swap_device = {"gx": core * blocks + low, "gy": path * 2 + high}
    core_device = {"gx": gx, "gy": path * 2 + 1 - core}

    def bit_device(b):
        return {"gx": high * blocks + flip_bit(low, b), "gy": gy}

    def sum_device(o):
        c = 1 - core if o >> bits & 1 else core
        return {"gx": high * blocks + flip_bits(low, o % blocks), "gy": path * 2 + c}

    def mark_device(o):
        h = 1 - high if o & 1 else high
        return {"gx": h * blocks + low, "gy": lax.rem(path + (o >> 1), paths) * 2 + core}

    def remote(src, dst, send, recv, device):
        return pltpu.make_async_remote_copy(
            src_ref=src, dst_ref=dst, send_sem=send, recv_sem=recv, device_id=device, device_id_type=MESH
        )

    def rows_of(p):
        return pl.ds(p * piece if isinstance(p, int) else pl.multiple_of(p * piece, piece), piece)

    @pl.when(home)
    def _():
        for p in range(PIECES):
            pltpu.make_async_copy(state.at[rows_of(p)], even.at[0, rows_of(p)], own_sem.at[p]).start()
        pltpu.make_async_copy(noise, kicks, noise_sem).start()

    @pl.when(away)
    def _():
        remote(noise, kicks, noise_send, noise_sem, swap_device).start()
        for p in range(PIECES):
            remote(
                state.at[rows_of(p)], even.at[0, rows_of(p)], swap_send, own_sem.at[p], swap_device
            ).start()

    place_a = lax.broadcasted_iota(jnp.int32, (SIDE, SIDE), 0)
    place_b = lax.broadcasted_iota(jnp.int32, (SIDE, SIDE), 1)
    distance = place_a ^ place_b
    flips = jnp.zeros((SIDE, SIDE), f32)
    for k in range(1, SIDE_BITS):
        flips = jnp.where(distance == 1 << k, fields[6 + k], flips)
    row_flips[0] = flips.astype(jnp.bfloat16)
    row_flips[1] = (flips - flips.astype(jnp.bfloat16).astype(f32)).astype(jnp.bfloat16)
    flips = jnp.where(distance == LANES, fields[6 + SIDE_BITS], jnp.zeros((SIDE, SIDE), f32))
    for q in range(LANE_BITS):
        flips = jnp.where(distance == 1 << q, fields[q], flips)
    pair_flips[0] = flips.astype(jnp.bfloat16)
    pair_flips[1] = (flips - flips.astype(jnp.bfloat16).astype(f32)).astype(jnp.bfloat16)

    row_ids = lax.broadcasted_iota(jnp.int32, (SIDE, LANES), 0)
    lane_ids = lax.broadcasted_iota(jnp.int32, (SIDE, LANES), 1)
    inner_bits = [lane_ids >> q & 1 for q in range(LANE_BITS)]
    inner_bits += [row_ids >> k & 1 for k in range(1, SIDE_BITS)]
    inner_count = len(inner_bits)
    inner_energy = jnp.zeros((SIDE, LANES), f32)
    inner_ones = jnp.zeros((SIDE, LANES), jnp.int32)
    for q in range(inner_count):
        inner_ones = inner_ones + inner_bits[q]
        if q + 1 < inner_count:
            inner_energy = inner_energy + couplings[q] * (spin(inner_bits[q]) * spin(inner_bits[q + 1]))
    table[0] = inner_energy
    table[1] = inner_ones.astype(f32) * (1.0 / spins)

    chunk_qubits = row_bits - chunk_bits
    top_spin = spin(core)
    low_spins = [spin(bit_of(low, b)) for b in range(bits)]

    def fill(k, carry):
        ids = [bit_of(k, t) for t in range(chunk_qubits)]
        z = [spin(b) for b in ids]
        count = ids[0]
        for b in ids[1:]:
            count = count + b
        energy = f32(0.0)
        for t in range(chunk_qubits - 1):
            energy = energy + couplings[inner_count + 1 + t] * (z[t] * z[t + 1])
        edge[k] = couplings[inner_count] * z[0]
        for j in range(blocks):
            zb = [low_spins[b] * (-1.0 if j >> b & 1 else 1.0) for b in range(bits)] + [top_spin]
            ones_j = count + core
            for b in range(bits):
                ones_j = ones_j + (1 - bit_of(low, b) if j >> b & 1 else bit_of(low, b))
            e = energy + couplings[spins - 2 - bits] * (z[-1] * zb[0])
            for b in range(bits):
                e = e + couplings[spins - 1 - bits + b] * (zb[b] * zb[b + 1])
            outer_energy[j * chunks + k] = e
            outer_ones[j * chunks + k] = ones_j.astype(f32) * (1.0 / spins)
        return carry

    lax.fori_loop(0, chunks, fill, 0)

    sub = lax.broadcasted_iota(jnp.int32, (8, LANES), 0)
    imag = (sub & 1) == 1
    lane_edge = spin(lax.broadcasted_iota(jnp.int32, (8, LANES), 1) & 1) * (couplings[spins - 1] * top_spin)

    def start_sums(s, norm, tilt):
        sums[s, 0, :8] = norm
        sums[s, 0, 8:] = tilt
        for o in range(1, 2 * blocks):
            remote(
                sums.at[s, 0], sums.at[s, o], sum_send.at[s], sum_recv.at[s], sum_device(o)
            ).start()

    def finish_sums(s):
        others = sums.at[s, pl.ds(1, 2 * blocks - 1)]
        wait_bytes(others, sum_recv.at[s])
        wait_bytes(others, sum_send.at[s])
        total = sums[s, 0]
        for o in range(1, 2 * blocks):
            total = total + sums[s, o]
        norm = jnp.full((8, LANES), jnp.sum(total[:8]), f32)
        tilt = jnp.full((8, LANES), jnp.sum(total[8:]), f32)
        return norm, tilt

    zero = jnp.zeros((8, LANES), f32)

    def first_sums():
        def body(k, carry):
            norm, tilt = carry
            for side in range(2):
                base = pl.multiple_of(k * CHUNK + side * SIDE, SIDE)
                x = even[0, pl.ds(base, SIDE), :]
                w = x * x
                ones = table[1] + (outer_ones[k] + side / spins)
                norm = norm + jnp.sum(w.reshape(groups, 8, LANES), axis=0)
                tilt = tilt + jnp.sum((w * ones).reshape(groups, 8, LANES), axis=0)
            return norm, tilt

        return lax.fori_loop(0, chunks, body, (zero, zero))

    def step_values(s):
        norm, tilt = finish_sums(s)
        magnet = tilt / norm
        factor = jnp.sqrt(f32(rows * (LANES // 2) * 2 * blocks) / norm)
        half_root = jnp.sqrt(jnp.full((8, LANES), DT / 2.0, f32))
        root_kappa = jnp.sqrt(jnp.full((8, LANES), KAPPA, f32))
        first = kicks[pl.ds(2 * s, 1), :] * half_root
        second = kicks[pl.ds(2 * s + 1, 1), :] * half_root
        drift = root_kappa * magnet * DT
        marks[0, pl.ds(2 * s, 1), :] = (drift + first)[:1]
        marks[0, pl.ds(2 * s + 1, 1), :] = (drift + second)[:1]
        ratio = root_kappa * second * (1.0 / DT)
        damp = factor * (DT * KAPPA * 0.5)
        table[2] = table[0] + (ratio.reshape(1, 8, LANES) * table[1].reshape(groups, 8, LANES)).reshape(SIDE, LANES)
        rate = factor * DT
        return dict(
            magnet=magnet, factor=factor, kick=factor * root_kappa * first, damp=damp, ratio=ratio,
            rate=jnp.where(imag, -rate, rate),
        )

    def flip_tile(src, j, k):
        x = jnp.concatenate(
            [bufs[src][j, pl.ds(pl.multiple_of(k * CHUNK + side * SIDE, SIDE), SIDE), :] for side in range(2)],
            axis=1,
        )
        coarse = x.astype(jnp.bfloat16)
        fine = (x - coarse.astype(f32)).astype(jnp.bfloat16)
        left = jnp.concatenate([row_flips[0], row_flips[0], row_flips[1], coarse, fine, coarse], axis=1)
        right = jnp.concatenate([coarse, fine, coarse, pair_flips[0], pair_flips[0], pair_flips[1]], axis=0)
        return jnp.dot(left, right, preferred_element_type=f32)

    base_ones = table[1, :8]

    def finish(src, j, k, tile, values, carry):
        here, there = bufs[src], bufs[1 - src]
        ones = outer_ones[j * chunks + k]
        keeps = []
        for n in range(SIDE_BITS - 1):
            shift = base_ones + (ones + n / spins - values["magnet"])
            keeps.append(values["factor"] + shift * (values["kick"] - values["damp"] * shift))
        level = lane_edge + outer_energy[j * chunks + k]
        weights = [None] * (SIDE_BITS - 1)
        for side in range(2):
            shift = ones + side / spins - values["magnet"]
            base_level = level + values["ratio"] * shift + (-edge[k] if side else edge[k])
            link = -couplings[inner_count - 1] if side else couplings[inner_count - 1]
            for part in range(SIDE // PART):
                offset = k * CHUNK + side * SIDE + part * PART
                rows_here = pl.ds(pl.multiple_of(offset, PART), PART)
                x = here[j, rows_here, :]
                total = tile[part * PART : (part + 1) * PART, side * LANES : (side + 1) * LANES]
                for t in range(chunk_bits, row_bits):
                    moved = flip_bit(k, t - chunk_bits) * CHUNK + side * SIDE + part * PART
                    total = total + fields[6 + t] * here[j, pl.ds(pl.multiple_of(moved, PART), PART), :]
                for b in range(bits):
                    total = total + fields[6 + row_bits + b] * here[other_block(j, b), rows_here, :]
                total = total + fields[spins - 1] * far[j, rows_here, :]
                top = part * PART * 2 // SIDE
                side_level = base_level - link if top else base_level + link
                x3 = x.reshape(part_groups, 8, LANES)
                diagonal = table[2, part * PART : (part + 1) * PART].reshape(part_groups, 8, LANES) + side_level[None]
                turned = values["rate"] * (total.reshape(part_groups, 8, LANES) + x3 * diagonal)
                turned = jnp.where(imag[None], pltpu.roll(turned, 1, 1), pltpu.roll(turned, 7, 1))
                counts = [ones_in(part * part_groups + g) + side for g in range(part_groups)]
                keep = jnp.concatenate([keeps[n][None] for n in counts], axis=0)
                new = keep * x3 + turned
                there[j, rows_here, :] = new.reshape(PART, LANES)
                if carry is not None:
                    w = new * new
                    for g, n in enumerate(counts):
                        weights[n] = w[g] if weights[n] is None else weights[n] + w[g]
        if carry is None:
            return None
        norm, tilt = carry
        some, scaled = weights[0], None
        for n in range(1, SIDE_BITS - 1):
            some = some + weights[n]
            scaled = weights[n] * (n / spins) if scaled is None else scaled + weights[n] * (n / spins)
        return norm + some, tilt + scaled + (base_ones + ones) * some

    def update(src, j, begin, end, values, sums_too, carry=None):
        ahead[...] = flip_tile(src, j, begin)

        def body(m, carry):
            k = begin + 2 * m
            later[...] = flip_tile(src, j, k + 1)
            carry = finish(src, j, k, ahead, values, carry)
            ahead[...] = flip_tile(src, j, jnp.minimum(k + 2, end - 1))
            return finish(src, j, k + 1, later, values, carry)

        trips = lax.div(end - begin, 2)
        if not sums_too:
            def plain(m, nothing):
                body(m, None)
                return nothing

            lax.fori_loop(0, trips, plain, 0)
            return None
        return lax.fori_loop(0, trips, body, carry or (zero, zero))

    def send_far(src, j, where=None):
        where = pl.ds(0, rows) if where is None else where
        remote(
            bufs[src].at[j, where], far.at[j, where], far_send.at[j], far_recv.at[j], core_device
        ).start()

    order = sorted(range(blocks), key=lambda j: (ones_in(j), j))
    levels = [[j for j in order if ones_in(j) == n] for n in range(bits + 1)]

    def last_hop(j, p):
        on = [b for b in range(bits) if j >> b & 1]
        return on[-1] if p % 4 == 3 else on[(p // 4) % (len(on) - 1)]

    def arrived(j, p):
        wait_bytes(even.at[j, rows_of(p)], arrive.at[j, p])
        send_far(0, j, rows_of(p))
        for b in range(bits):
            target = j | 1 << b
            if not j >> b & 1 and last_hop(target, p) == b:
                remote(
                    even.at[j, rows_of(p)], even.at[target, rows_of(p)],
                    relay_send.at[target], arrive.at[target, p], bit_device(b),
                ).start()

    lag = 2
    for p in range(PIECES):
        wait_bytes(even.at[0, rows_of(p)], own_sem.at[p])
        for b in range(bits):
            remote(
                even.at[0, rows_of(p)], even.at[1 << b, rows_of(p)],
                push_send.at[b], arrive.at[1 << b, p], bit_device(b),
            ).start()
        send_far(0, 0, rows_of(p))
        if p >= lag:
            for j in levels[1]:
                arrived(j, p - lag)
    start_sums(0, *first_sums())
    for p in range(PIECES - lag, PIECES):
        for j in levels[1]:
            arrived(j, p)
    wait_bytes(kicks, noise_sem)

    values = step_values(0)
    everything = pl.ds(0, rows)

    def far_ready(j):
        wait_bytes(far.at[j, everything], far_recv.at[j])

    def whole(src, j, sums_too):
        far_ready(j)
        return update(src, j, 0, chunks, values, sums_too)

    for n in range(2, bits + 1):
        for j in levels[n - 2]:
            got = whole(0, j, j == 0)
            if j == 0:
                start_sums(1, *got)
        if n < bits:
            for p in range(PIECES):
                for j in levels[n]:
                    arrived(j, p)
    last = blocks - 1

    def late_block(t, carry):
        final = t == 2 * bits
        half = lax.div(t, bits)

        @pl.when((lax.rem(t, bits) == 0) & (t < 2 * bits))
        def _():
            def take(p, nothing):
                arrived(last, half * (PIECES // 2) + p)
                return nothing

            lax.fori_loop(0, PIECES // 2, take, 0)

        j = last - jnp.where(final, 0, lax.shift_left(1, lax.rem(t, bits)))

        @pl.when((t < bits) | final)
        def _():
            far_ready(j)

        begin = jnp.where(final, 0, half * (chunks // 2))
        end = jnp.where(final, chunks, (half + 1) * (chunks // 2))
        update(0, j, begin, end, values, False)
        return carry

    lax.fori_loop(0, 2 * bits + 1, late_block, 0)

    @pl.when(away)
    def _():
        wait_bytes(state, swap_send)
        wait_bytes(noise, noise_send)

    for b in range(bits):
        wait_bytes(even.at[0], push_send.at[b])
    for j in order:
        if ones_in(j) >= 2:
            wait_bytes(even.at[j], relay_send.at[j])

    def send_next(src, j):
        pl.semaphore_wait(free.at[j], 1)
        wait_bytes(bufs[src].at[j], far_send.at[j])
        send_far(src, j)

    def release(j):
        pl.semaphore_signal(free.at[j], 1, device_id=core_device, device_id_type=MESH)

    def needed(s):
        return [j for j in range(blocks) if ones_in(j) <= steps - 1 - s]

    def is_needed(j, s):
        count = bit_of(j, 0)
        for b in range(1, bits):
            count = count + bit_of(j, b)
        return count <= steps - 1 - s

    for j in needed(1):
        release(j)
    for j in needed(1):
        send_next(1, j)

    for s in range(1, steps - 1):
        src = s % 2
        values = step_values(s)
        start_sums(s + 1, *whole(src, 0, True))
        release(0)
        previous = 0
        rest = needed(s)[1:]
        while rest:
            first = stop = rest[0]
            while stop in rest:
                stop += 1
            rest = [j for j in rest if j >= stop]

            def one_block(j, carry, first=first, previous=previous, src=src, s=s, values=values):
                far_ready(j)
                update(src, j, 0, chunks, values, False)

                @pl.when(is_needed(j, s + 1))
                def _():
                    release(j)

                before = jnp.where(j == first, previous, j - 1)

                @pl.when(is_needed(before, s + 1))
                def _():
                    send_next(1 - src, before)

                return carry

            lax.fori_loop(first, stop, one_block, 0)
            previous = stop - 1
        if previous in needed(s + 1):
            send_next(1 - src, previous)

    src = (steps - 1) % 2
    values = step_values(steps - 1)
    for o in range(1, 2 * paths):
        remote(marks.at[0], marks.at[o], mark_send, mark_recv, mark_device(o)).start()
    far_ready(0)

    def deliver(p):
        @pl.when(home)
        def _():
            pltpu.make_async_copy(bufs[1 - src].at[0, rows_of(p)], out.at[rows_of(p)], out_sem).start()

        @pl.when(away)
        def _():
            remote(
                bufs[1 - src].at[0, rows_of(p)], out.at[rows_of(p)], out_send, out_sem, swap_device
            ).start()

    def last_piece(p, carry):
        update(src, 0, p * piece_chunks, (p + 1) * piece_chunks, values, False)

        @pl.when(p > 0)
        def _():
            deliver(p - 1)

        return carry

    lax.fori_loop(0, PIECES, last_piece, 0)
    deliver(PIECES - 1)

    others = marks.at[pl.ds(1, 2 * paths - 1)]
    wait_bytes(others, mark_recv)
    wait_bytes(others, mark_send)
    total = marks[0]
    for o in range(1, 2 * paths):
        total = total + marks[o]
    record[...] = total
    for j in order:
        wait_bytes(even.at[j], far_send.at[j])
    wait_bytes(out, out_sem)

    @pl.when(away)
    def _():
        wait_bytes(out, out_send)


def shards(state, fields, couplings, noise):
    local_len = state.shape[2]
    steps = noise.shape[1]
    bits = lax.axis_size("gx").bit_length() - 2
    paths = lax.axis_size("gy") // 2
    spins = local_len.bit_length() - 1 + bits + 1
    blocks = 1 << bits
    rows = 2 * local_len // LANES
    chunks = rows // CHUNK
    f32 = jnp.float32
    mixed = state.reshape(2, rows // 2, LANES).transpose(1, 0, 2).reshape(rows, LANES)
    kicks = jnp.broadcast_to(noise.reshape(steps * 2, 1), (steps * 2, LANES))
    smem = pl.BlockSpec(memory_space=pltpu.SMEM)
    hbm = pl.BlockSpec(memory_space=pl.ANY)
    dma, regular = pltpu.SemaphoreType.DMA, pltpu.SemaphoreType.REGULAR
    tile = (steps * 2, LANES)
    out, record = pl.pallas_call(
        functools.partial(evolve_kernel, bits, paths, steps, spins),
        in_specs=[smem, smem, hbm, hbm],
        out_specs=[hbm, pl.BlockSpec(memory_space=pltpu.VMEM)],
        out_shape=[jax.ShapeDtypeStruct((rows, LANES), f32), jax.ShapeDtypeStruct(tile, f32)],
        scratch_shapes=[
            pltpu.VMEM((blocks, rows, LANES), f32),
            pltpu.VMEM((blocks, rows, LANES), f32),
            pltpu.VMEM((blocks, rows, LANES), f32),
            pltpu.VMEM((2, SIDE, SIDE), jnp.bfloat16),
            pltpu.VMEM((2, SIDE, SIDE), jnp.bfloat16),
            pltpu.VMEM((SIDE, SIDE), f32),
            pltpu.VMEM((SIDE, SIDE), f32),
            pltpu.VMEM((3, SIDE, LANES), f32),
            pltpu.SMEM((blocks * chunks,), f32),
            pltpu.SMEM((blocks * chunks,), f32),
            pltpu.SMEM((chunks,), f32),
            pltpu.VMEM((steps, 2 * blocks, 16, LANES), f32),
            pltpu.VMEM((2 * paths,) + tile, f32),
            pltpu.VMEM(tile, f32),
            dma((PIECES,)), dma, dma, dma, dma((blocks, PIECES)), dma((bits,)), dma((blocks,)),
            dma((blocks,)), dma((blocks,)), dma((steps,)), dma((steps,)), dma, dma, dma, dma,
            regular((blocks,)),
        ],
        compiler_params=pltpu.CompilerParams(has_side_effects=True, vmem_limit_bytes=60 << 20),
    )(fields, couplings, kicks, mixed)
    final = out.reshape(rows // 2, 2, LANES).transpose(1, 0, 2).reshape(1, 2, local_len)
    return final, record[:, 0].reshape(steps, 2)


def solution(mesh):
    placed = (P("gy", None, "gx"), P(), P(), P("gy", None, None))
    return jax.shard_map(
        shards, mesh=mesh, in_specs=placed, out_specs=(P("gy", None, "gx"), P()), check_vma=False
    )
```

time: 434 us -> 362 us (0.83)
  Pallas kernels: 425 us -> 353 us
    pallas_call x1, Pallas kernels: 425 us -> 353 us  [shards(): pl.pallas_call(functools.partial(evolve_kernel, bits, paths, steps, spins...]
where the time goes in v2:
time: 362 us
  Pallas kernels  353 us (98%)
  local copies, waits for them, and re-layouts  7.78 us (2%)
    pallas_call x1, Pallas kernels, shards(): pl.pallas_call(functools.partial(evolve_kernel, bits, paths, steps, spins...  353 us

profile of v2, /device:TPU:1, one launch (start us, length us, event | category | flops | bytes accessed | tf_op | source)
XLA Modules:
  0.0 361.8 jit_solution(15153258384293190184)
XLA Ops:
  0.6 0.8 copy.10
  1.4 0.1 broadcast_in_dim.7
  1.5 0.7 broadcast_in_dim.8.noise
  2.1 353.4 %shard_map.59 = (f32[8192,128]{1,0:T(8,128)}, f32[8,128]{1,0:T(8,128)}) custom-call(f32[22]{0:T(128)} %fields.1, f32[22]{0:T(128)} %couplings.1, f32[8,128]{1,0:T(8,128)} %broadcast_in_dim.8.noise, f32[8192,128]{1,0:T(8,128)} %bitcast.10), custom_call_target="tpu_custom_call" | custom-call | tf_op jit(solution)/shard_map/pallas_call | solution.py:526
  355.5 0.8 slice_reduce_fusion
  356.3 0.1 reshape_squeeze.3
  356.4 0.7 copy.13
  357.1 4.7 %copy.15 = f32[1,2,524288]{2,1,0:T(2,128)} copy(f32[1,2,524288]{2,1,0:T(2,128)} %bitcast.11) | data formatting | bytes 8388608

commit v3 on v2

--- a/solution.py
+++ b/solution.py
@@ -307,18 +307,40 @@
             return None
         return lax.fori_loop(0, trips, body, carry or (zero, zero))
 
+    everything = pl.ds(0, rows)
+
+    def far_ready(j):
+        wait_bytes(far.at[j, everything], far_recv.at[j])
+
     def send_far(src, j, where=None):
         where = pl.ds(0, rows) if where is None else where
         remote(
             bufs[src].at[j, where], far.at[j, where], far_send.at[j], far_recv.at[j], core_device
         ).start()
 
+    def send_next(src, j):
+        pl.semaphore_wait(free.at[j], 1)
+        wait_bytes(bufs[src].at[j], far_send.at[j])
+        send_far(src, j)
+
+    def release(j):
+        pl.semaphore_signal(free.at[j], 1, device_id=core_device, device_id_type=MESH)
+
+    def needed(s):
+        return [j for j in range(blocks) if ones_in(j) <= steps - 1 - s]
+
+    def is_needed(j, s):
+        count = bit_of(j, 0)
+        for b in range(1, bits):
+            count = count + bit_of(j, b)
+        return count <= steps - 1 - s
+
     order = sorted(range(blocks), key=lambda j: (ones_in(j), j))
     levels = [[j for j in order if ones_in(j) == n] for n in range(bits + 1)]
 
     def last_hop(j, p):
         on = [b for b in range(bits) if j >> b & 1]
-        return on[-1] if p % 4 == 3 else on[(p // 4) % (len(on) - 1)]
+        return on[-1] if 4 * p >= 3 * PIECES else on[p % (len(on) - 1)]
 
     def arrived(j, p):
         wait_bytes(even.at[j, rows_of(p)], arrive.at[j, p])
@@ -331,39 +353,45 @@
                     relay_send.at[target], arrive.at[target, p], bit_device(b),
                 ).start()
 
-    lag = 2
+    def push(b, p):
+        remote(
+            even.at[0, rows_of(p)], even.at[1 << b, rows_of(p)],
+            push_send.at[b], arrive.at[1 << b, p], bit_device(b),
+        ).start()
+
+    crossed = bit_of(low, bits - 1) != high
     for p in range(PIECES):
         wait_bytes(even.at[0, rows_of(p)], own_sem.at[p])
-        for b in range(bits):
-            remote(
-                even.at[0, rows_of(p)], even.at[1 << b, rows_of(p)],
-                push_send.at[b], arrive.at[1 << b, p], bit_device(b),
-            ).start()
+        for b in range(bits - 1):
+            push(b, p)
+        pl.when(away | jnp.logical_not(crossed))(functools.partial(push, bits - 1, p))
         send_far(0, 0, rows_of(p))
-        if p >= lag:
-            for j in levels[1]:
-                arrived(j, p - lag)
     start_sums(0, *first_sums())
-    for p in range(PIECES - lag, PIECES):
-        for j in levels[1]:
+    far_ready(0)
+
+    @pl.when(home & crossed)
+    def _():
+        for p in range(PIECES):
+            push(bits - 1, p)
+
+    for j in reversed(levels[1]):
+        for p in range(PIECES):
             arrived(j, p)
     wait_bytes(kicks, noise_sem)
 
     values = step_values(0)
-    everything = pl.ds(0, rows)
-
-    def far_ready(j):
-        wait_bytes(far.at[j, everything], far_recv.at[j])
-
     def whole(src, j, sums_too):
         far_ready(j)
         return update(src, j, 0, chunks, values, sums_too)
 
+    start_sums(1, *update(0, 0, 0, chunks, values, True))
+    release(0)
     for n in range(2, bits + 1):
         for j in levels[n - 2]:
-            got = whole(0, j, j == 0)
-            if j == 0:
-                start_sums(1, *got)
+            if j:
+                whole(0, j, False)
+                release(j)
+                send_next(1, j)
         if n < bits:
             for p in range(PIECES):
                 for j in levels[n]:
@@ -391,9 +419,24 @@
         begin = jnp.where(final, 0, half * (chunks // 2))
         end = jnp.where(final, chunks, (half + 1) * (chunks // 2))
         update(0, j, begin, end, values, False)
+
+        @pl.when((t >= bits) & is_needed(j, 1))
+        def _():
+            release(j)
+
+        @pl.when(t == 0)
+        def _():
+            send_next(1, 0)
+
+        @pl.when((t > bits) & is_needed(last - 1, 1))
+        def _():
+            send_next(1, last - lax.shift_left(1, lax.rem(t - 1, bits)))
+
         return carry
 
     lax.fori_loop(0, 2 * bits + 1, late_block, 0)
+    if last in needed(1):
+        send_next(1, last)
 
     @pl.when(away)
     def _():
@@ -405,28 +448,6 @@
     for j in order:
         if ones_in(j) >= 2:
             wait_bytes(even.at[j], relay_send.at[j])
-
-    def send_next(src, j):
-        pl.semaphore_wait(free.at[j], 1)
-        wait_bytes(bufs[src].at[j], far_send.at[j])
-        send_far(src, j)
-
-    def release(j):
-        pl.semaphore_signal(free.at[j], 1, device_id=core_device, device_id_type=MESH)
-
-    def needed(s):
-        return [j for j in range(blocks) if ones_in(j) <= steps - 1 - s]
-
-    def is_needed(j, s):
-        count = bit_of(j, 0)
-        for b in range(1, bits):
-            count = count + bit_of(j, b)
-        return count <= steps - 1 - s
-
-    for j in needed(1):
-        release(j)
-    for j in needed(1):
-        send_next(1, j)
 
     for s in range(1, steps - 1):
         src = s % 2

time: 362 us -> 349 us (0.964)
  Pallas kernels: 353 us -> 341 us
    pallas_call x1, Pallas kernels: 353 us -> 341 us  [shards(): pl.pallas_call(functools.partial(evolve_kernel, bits, paths, steps, spins...]
where the time goes in v3:
time: 349 us
  Pallas kernels  341 us (98%)
  local copies, waits for them, and re-layouts  7.78 us (2%)
    pallas_call x1, Pallas kernels, shards(): pl.pallas_call(functools.partial(evolve_kernel, bits, paths, steps, spins...  341 us

profile of v3, /device:TPU:1, one launch (start us, length us, event | category | flops | bytes accessed | tf_op | source)
XLA Modules:
  0.0 349.2 jit_solution(15054855816795646758)
XLA Ops:
  0.6 0.8 copy.10
  1.4 0.1 broadcast_in_dim.7
  1.5 0.7 broadcast_in_dim.8.noise
  2.1 340.8 %shard_map.59 = (f32[8192,128]{1,0:T(8,128)}, f32[8,128]{1,0:T(8,128)}) custom-call(f32[22]{0:T(128)} %fields.1, f32[22]{0:T(128)} %couplings.1, f32[8,128]{1,0:T(8,128)} %broadcast_in_dim.8.noise, f32[8192,128]{1,0:T(8,128)} %bitcast.10), custom_call_target="tpu_custom_call" | custom-call | tf_op jit(solution)/shard_map/pallas_call | solution.py:547
  342.9 0.8 slice_reduce_fusion
  343.7 0.1 reshape_squeeze.3
  343.8 0.7 copy.13
  344.5 4.7 %copy.15 = f32[1,2,524288]{2,1,0:T(2,128)} copy(f32[1,2,524288]{2,1,0:T(2,128)} %bitcast.11) | data formatting | bytes 8388608

commit v4 on v3

--- a/solution.py
+++ b/solution.py
@@ -15,7 +15,9 @@
 SIDE_BITS = 8
 CHUNK = 2 * SIDE
 PART = 64
-PIECES = 8
+PIECES = 16
+QUARTERS = 4
+DELIVERIES = 8
 MESH = pl.DeviceIdType.MESH
 
 
@@ -55,7 +57,7 @@
 def evolve_kernel(
     bits, paths, steps, spins,
     fields, couplings, noise, state, out, record,
-    even, odd, far, row_flips, pair_flips, ahead, later, table, outer_energy, outer_ones, edge, sums, marks, kicks,
+    even, odd, far, row_flips, pair_flips, near_parts, next_parts, ahead, later, table, outer_energy, outer_ones, edge, sums, marks, kicks,
     own_sem, swap_send, noise_sem, noise_send, arrive, push_send, relay_send,
     far_send, far_recv, sum_send, sum_recv, mark_send, mark_recv, out_sem, out_send, free,
 ):
@@ -67,7 +69,8 @@
     bufs = (even, odd)
     chunks = rows // CHUNK
     piece = rows // PIECES
-    piece_chunks = piece // CHUNK
+    delivery = rows // DELIVERIES
+    delivery_chunks = delivery // CHUNK
     groups = SIDE // 8
     part_groups = PART // 8
 
@@ -97,6 +100,9 @@
 
     def rows_of(p):
         return pl.ds(p * piece if isinstance(p, int) else pl.multiple_of(p * piece, piece), piece)
+
+    def delivery_of(p):
+        return pl.ds(p * delivery if isinstance(p, int) else pl.multiple_of(p * delivery, delivery), delivery)
 
     @pl.when(home)
     def _():
@@ -227,16 +233,28 @@
             rate=jnp.where(imag, -rate, rate),
         )
 
-    def flip_tile(src, j, k):
-        x = jnp.concatenate(
-            [bufs[src][j, pl.ds(pl.multiple_of(k * CHUNK + side * SIDE, SIDE), SIDE), :] for side in range(2)],
-            axis=1,
+    def split(src, j, k, parts):
+        k = jnp.minimum(k, chunks - 1)
+        for side in range(2):
+            x = bufs[src][j, pl.ds(pl.multiple_of(k * CHUNK + side * SIDE, SIDE), SIDE), :]
+            coarse = x.astype(jnp.bfloat16)
+            parts[0, :, side * LANES : (side + 1) * LANES] = coarse
+            parts[1, :, side * LANES : (side + 1) * LANES] = (x - coarse.astype(f32)).astype(jnp.bfloat16)
+
+    def flip_tile(parts, held=None):
+        left = [parts[0], parts[1], parts[0], row_flips[0], row_flips[0], row_flips[1]]
+        right = [pair_flips[0], pair_flips[0], pair_flips[1], parts[0], parts[1], parts[0]]
+        if held is not None:
+            for i in range(1, len(right)):
+                right[i] = jnp.concatenate([right[i][:16] + held[i - 1], right[i][16:]], axis=0)
+        return jnp.dot(
+            jnp.concatenate(left, axis=1), jnp.concatenate(right, axis=0), preferred_element_type=f32
         )
-        coarse = x.astype(jnp.bfloat16)
-        fine = (x - coarse.astype(f32)).astype(jnp.bfloat16)
-        left = jnp.concatenate([row_flips[0], row_flips[0], row_flips[1], coarse, fine, coarse], axis=1)
-        right = jnp.concatenate([coarse, fine, coarse, pair_flips[0], pair_flips[0], pair_flips[1]], axis=0)
-        return jnp.dot(left, right, preferred_element_type=f32)
+
+    def hold(new):
+        zeros = jnp.minimum(jnp.abs(new), 0.0)
+        zeros = jnp.concatenate([zeros, zeros], axis=0).astype(jnp.bfloat16)
+        return jnp.concatenate([zeros, zeros], axis=1)
 
     base_ones = table[1, :8]
 
@@ -249,6 +267,7 @@
             keeps.append(values["factor"] + shift * (values["kick"] - values["damp"] * shift))
         level = lane_edge + outer_energy[j * chunks + k]
         weights = [None] * (SIDE_BITS - 1)
+        held = []
         for side in range(2):
             shift = ones + side / spins - values["magnet"]
             base_level = level + values["ratio"] * shift + (-edge[k] if side else edge[k])
@@ -274,28 +293,40 @@
                 keep = jnp.concatenate([keeps[n][None] for n in counts], axis=0)
                 new = keep * x3 + turned
                 there[j, rows_here, :] = new.reshape(PART, LANES)
+                lowest = new[0]
+                for g in range(1, part_groups):
+                    lowest = jnp.minimum(lowest, new[g])
+                held.append(hold(lowest))
                 if carry is not None:
                     w = new * new
                     for g, n in enumerate(counts):
                         weights[n] = w[g] if weights[n] is None else weights[n] + w[g]
         if carry is None:
-            return None
+            return None, held
         norm, tilt = carry
         some, scaled = weights[0], None
         for n in range(1, SIDE_BITS - 1):
             some = some + weights[n]
             scaled = weights[n] * (n / spins) if scaled is None else scaled + weights[n] * (n / spins)
-        return norm + some, tilt + scaled + (base_ones + ones) * some
+        return (norm + some, tilt + scaled + (base_ones + ones) * some), held
 
     def update(src, j, begin, end, values, sums_too, carry=None):
-        ahead[...] = flip_tile(src, j, begin)
+        split(src, j, begin, near_parts)
+        split(src, j, begin + 1, next_parts)
+        ahead[...] = flip_tile(near_parts)
+        later[...] = flip_tile(next_parts)
+        split(src, j, begin + 2, near_parts)
+        split(src, j, begin + 3, next_parts)
 
         def body(m, carry):
             k = begin + 2 * m
-            later[...] = flip_tile(src, j, k + 1)
-            carry = finish(src, j, k, ahead, values, carry)
-            ahead[...] = flip_tile(src, j, jnp.minimum(k + 2, end - 1))
-            return finish(src, j, k + 1, later, values, carry)
+            carry, held = finish(src, j, k, ahead, values, carry)
+            ahead[...] = flip_tile(near_parts, held)
+            split(src, j, k + 4, near_parts)
+            carry, held = finish(src, j, k + 1, later, values, carry)
+            later[...] = flip_tile(next_parts, held)
+            split(src, j, k + 5, next_parts)
+            return carry
 
         trips = lax.div(end - begin, 2)
         if not sums_too:
@@ -399,16 +430,16 @@
     last = blocks - 1
 
     def late_block(t, carry):
-        final = t == 2 * bits
-        half = lax.div(t, bits)
-
-        @pl.when((lax.rem(t, bits) == 0) & (t < 2 * bits))
+        final = t == QUARTERS * bits
+        quarter = lax.div(t, bits)
+
+        @pl.when((lax.rem(t, bits) == 0) & (t < QUARTERS * bits))
         def _():
             def take(p, nothing):
-                arrived(last, half * (PIECES // 2) + p)
+                arrived(last, quarter * (PIECES // QUARTERS) + p)
                 return nothing
 
-            lax.fori_loop(0, PIECES // 2, take, 0)
+            lax.fori_loop(0, PIECES // QUARTERS, take, 0)
 
         j = last - jnp.where(final, 0, lax.shift_left(1, lax.rem(t, bits)))
 
@@ -416,11 +447,11 @@
         def _():
             far_ready(j)
 
-        begin = jnp.where(final, 0, half * (chunks // 2))
-        end = jnp.where(final, chunks, (half + 1) * (chunks // 2))
+        begin = jnp.where(final, 0, quarter * (chunks // QUARTERS))
+        end = jnp.where(final, chunks, (quarter + 1) * (chunks // QUARTERS))
         update(0, j, begin, end, values, False)
 
-        @pl.when((t >= bits) & is_needed(j, 1))
+        @pl.when((t >= (QUARTERS - 1) * bits) & is_needed(j, 1))
         def _():
             release(j)
 
@@ -428,13 +459,13 @@
         def _():
             send_next(1, 0)
 
-        @pl.when((t > bits) & is_needed(last - 1, 1))
+        @pl.when((t > (QUARTERS - 1) * bits) & is_needed(last - 1, 1))
         def _():
             send_next(1, last - lax.shift_left(1, lax.rem(t - 1, bits)))
 
         return carry
 
-    lax.fori_loop(0, 2 * bits + 1, late_block, 0)
+    lax.fori_loop(0, QUARTERS * bits + 1, late_block, 0)
     if last in needed(1):
         send_next(1, last)
 
@@ -492,16 +523,16 @@
     def deliver(p):
         @pl.when(home)
         def _():
-            pltpu.make_async_copy(bufs[1 - src].at[0, rows_of(p)], out.at[rows_of(p)], out_sem).start()
+            pltpu.make_async_copy(bufs[1 - src].at[0, delivery_of(p)], out.at[delivery_of(p)], out_sem).start()
 
         @pl.when(away)
         def _():
             remote(
-                bufs[1 - src].at[0, rows_of(p)], out.at[rows_of(p)], out_send, out_sem, swap_device
+                bufs[1 - src].at[0, delivery_of(p)], out.at[delivery_of(p)], out_send, out_sem, swap_device
             ).start()
 
     def last_piece(p, carry):
-        update(src, 0, p * piece_chunks, (p + 1) * piece_chunks, values, False)
+        update(src, 0, p * delivery_chunks, (p + 1) * delivery_chunks, values, False)
 
         @pl.when(p > 0)
         def _():
@@ -509,8 +540,8 @@
 
         return carry
 
-    lax.fori_loop(0, PIECES, last_piece, 0)
-    deliver(PIECES - 1)
+    lax.fori_loop(0, DELIVERIES, last_piece, 0)
+    deliver(DELIVERIES - 1)
 
     others = marks.at[pl.ds(1, 2 * paths - 1)]
     wait_bytes(others, mark_recv)
@@ -555,6 +586,8 @@
             pltpu.VMEM((blocks, rows, LANES), f32),
             pltpu.VMEM((2, SIDE, SIDE), jnp.bfloat16),
             pltpu.VMEM((2, SIDE, SIDE), jnp.bfloat16),
+            pltpu.VMEM((2, SIDE, SIDE), jnp.bfloat16),
+            pltpu.VMEM((2, SIDE, SIDE), jnp.bfloat16),
             pltpu.VMEM((SIDE, SIDE), f32),
             pltpu.VMEM((SIDE, SIDE), f32),
             pltpu.VMEM((3, SIDE, LANES), f32),

time: 349 us -> 345 us (0.989)
  Pallas kernels: 341 us -> 336 us
    pallas_call x1, Pallas kernels: 341 us -> 336 us  [shards(): pl.pallas_call(functools.partial(evolve_kernel, bits, paths, steps, spins...]
where the time goes in v4:
time: 345 us; the launch traced here: 344 us
  Pallas kernels  336 us (97%)
  local copies, waits for them, and re-layouts  7.78 us (2%)
    pallas_call x1, Pallas kernels, shards(): pl.pallas_call(functools.partial(evolve_kernel, bits, paths, steps, spins...  336 us

profile of v4, /device:TPU:1, one launch (start us, length us, event | category | flops | bytes accessed | tf_op | source)
XLA Modules:
  0.0 344.3 jit_solution(2180149131946516992)
XLA Ops:
  0.6 0.8 copy.10
  1.4 0.1 broadcast_in_dim.7
  1.5 0.7 broadcast_in_dim.8.noise
  2.1 335.9 %shard_map.59 = (f32[8192,128]{1,0:T(8,128)}, f32[8,128]{1,0:T(8,128)}) custom-call(f32[22]{0:T(128)} %fields.1, f32[22]{0:T(128)} %couplings.1, f32[8,128]{1,0:T(8,128)} %broadcast_in_dim.8.noise, f32[8192,128]{1,0:T(8,128)} %bitcast.10), custom_call_target="tpu_custom_call" | custom-call | tf_op jit(solution)/shard_map/pallas_call | solution.py:578
  338.0 0.8 slice_reduce_fusion
  338.8 0.1 reshape_squeeze.3
  338.9 0.7 copy.13
  339.6 4.7 %copy.15 = f32[1,2,524288]{2,1,0:T(2,128)} copy(f32[1,2,524288]{2,1,0:T(2,128)} %bitcast.11) | data formatting | bytes 8388608
